TPU v7x, 128 devices: a whole 4x4x4 slice. The times are simulated.
128 devices in a mesh: dp: 4 (over z), col: 4 (over y), fsdp: 8 (over x, core).
Axes of the slice: x: 4, y: 4, z: 4, core: 2. Of those that a mesh axis runs over, the one named last changes fastest.
Arguments:
- x_act: bfloat16 [524288, 288], P(('dp', 'col', 'fsdp'))
- dy_out: bfloat16 [524288, 288], P(('dp', 'col', 'fsdp'))
- w_gate: bfloat16 [288, 768], P(None, ('col', 'fsdp'))
- w_up: bfloat16 [288, 768], P(None, ('col', 'fsdp'))
- w_down: bfloat16 [768, 288], P(('col', 'fsdp'))
- v_gate: bfloat16 [288, 768], P(None, ('col', 'fsdp'))
- v_up: bfloat16 [288, 768], P(None, ('col', 'fsdp'))
- v_down: bfloat16 [768, 288], P(('col', 'fsdp'))
- g_next: float32 [128, 3, 288, 768], P(('dp', 'col', 'fsdp'))
Outputs:
- output 1: bfloat16 [524288, 288], P(('dp', 'col', 'fsdp'))
- output 2: float32 [3, 288, 768], P(None, None, ('col', 'fsdp'))
- output 3: float32 [128, 3, 288, 768], P(('dp', 'col', 'fsdp'))
- output 4: bfloat16 [288, 768], replicated
- output 5: bfloat16 [288, 768], replicated
- output 6: bfloat16 [768, 288], replicated
All inputs are finite; a program needn't handle non-finite values.
Results may differ from a plain program's by a relative error of at most 0.0145327.
Values are sent between devices in bfloat16 or wider.
A program may use at most 1 GiB of HBM per device.

v0:
```python
import jax
import jax.numpy as jnp
from jax import lax
from jax.sharding import PartitionSpec as P

ALL_AXES = ('dp', 'col', 'fsdp')
FSDP_AXES = ('col', 'fsdp')


def local_backward(x_loc, dy_loc, gate_full, up_full, down_full):
    pre_gate = jnp.dot(x_loc, gate_full, preferred_element_type=jnp.float32)
    pre_up = jnp.dot(x_loc, up_full, preferred_element_type=jnp.float32)
    sig_gate = jax.nn.sigmoid(pre_gate)
    act_gate = pre_gate * sig_gate
    hidden = (act_gate * pre_up).astype(jnp.bfloat16)
    d_hidden = jnp.einsum('td,fd->tf', dy_loc, down_full, preferred_element_type=jnp.float32)
    d_gate = (d_hidden * pre_up * sig_gate * (1.0 + pre_gate * (1.0 - sig_gate))).astype(jnp.bfloat16)
    d_up = (d_hidden * act_gate).astype(jnp.bfloat16)
    dx_loc = (jnp.einsum('tf,df->td', d_gate, gate_full, preferred_element_type=jnp.float32)
              + jnp.einsum('tf,df->td', d_up, up_full, preferred_element_type=jnp.float32)).astype(jnp.bfloat16)
    grad_local = jnp.stack([
        jnp.einsum('td,tf->df', x_loc, d_gate, preferred_element_type=jnp.float32),
        jnp.einsum('td,tf->df', x_loc, d_up, preferred_element_type=jnp.float32),
        jnp.einsum('td,tf->df', dy_loc, hidden, preferred_element_type=jnp.float32),
    ])
    return dx_loc, grad_local


def solution(mesh):
    def device_step(x_loc, dy_loc, w_gate, w_up, w_down, v_gate, v_up, v_down, g_next):
        gate_full = lax.all_gather(w_gate, FSDP_AXES, axis=1, tiled=True)
        up_full = lax.all_gather(w_up, FSDP_AXES, axis=1, tiled=True)
        down_full = lax.all_gather(w_down, FSDP_AXES, axis=0, tiled=True)
        v_gate_full = lax.all_gather(v_gate, FSDP_AXES, axis=1, tiled=True)
        v_up_full = lax.all_gather(v_up, FSDP_AXES, axis=1, tiled=True)
        v_down_full = lax.all_gather(v_down, FSDP_AXES, axis=0, tiled=True)
        grad_shard = lax.psum_scatter(g_next[0].astype(jnp.bfloat16), FSDP_AXES, scatter_dimension=2, tiled=True)
        grad_next = lax.psum(grad_shard.astype(jnp.float32), 'dp')
        dx_loc, grad_local = local_backward(x_loc, dy_loc, gate_full, up_full, down_full)
        return dx_loc, grad_next, grad_local[None], v_gate_full, v_up_full, v_down_full

    row_spec = P(ALL_AXES, None)
    col_shard = P(None, FSDP_AXES)
    row_shard = P(FSDP_AXES, None)
    dev_spec = P(ALL_AXES, None, None, None)
    return jax.shard_map(
        device_step, mesh=mesh,
        in_specs=(row_spec, row_spec, col_shard, col_shard, row_shard, col_shard, col_shard, row_shard, dev_spec),
        out_specs=(row_spec, P(None, None, FSDP_AXES), dev_spec, P(), P(), P()),
        check_vma=False)
```

profile of v0, /device:TPU:1, one launch (start us, length us, event | category | flops | bytes accessed | tf_op | source)
XLA Modules:
  0.0 243.4 jit_solution(13776787660850030212)
XLA Ops:
  7.2 0.0 copy-start
  7.2 0.0 copy-start.4
  7.2 0.0 all-reduce.6.cloned.1.call-start
  7.2 3.1 %copy.19 = bf16[1,3,288,768]{2,3,1,0:T(8,128)(2,1)} copy(f32[1,3,288,768]{3,2,1,0:T(8,128)} %param.17) | data formatting | bytes 3981312 | tf_op args[8]
  10.3 0.0 all-reduce.6.cloned.1.call-update
  10.4 0.0 all-reduce.4.cloned.1.call-start
  10.4 26.6 %all_gather.19 = bf16[288,768]{0,1:T(8,128)(2,1)S(1)} all-gather(bf16[288,24]{0,1:T(8,128)(2,1)} %param.12), channel_id=1, replica_groups=mesh['dp'=4,'col'=4,'fsdp'=8] {'col','fsdp'}, dimensions={1}, use_global_device_ids=true | all-gather | bytes 456192 | tf_op jit(solution)/shard_map/all_gather | solution.py:32
  37.0 0.0 copy-done.4
  37.0 24.2 %all_gather.20 = bf16[288,768]{0,1:T(8,128)(2,1)S(1)} all-gather(bf16[288,24]{0,1:T(8,128)(2,1)S(1)} %copy-done.4), channel_id=1, replica_groups=mesh['dp'=4,'col'=4,'fsdp'=8] {'col','fsdp'}, dimensions={1}, use_global_device_ids=true | all-gather | bytes 456192 | tf_op jit(solution)/shard_map/all_gather | solution.py:31
  61.2 0.0 copy-done
  61.2 3.5 %fusion.6 = f32[4096,768]{1,0:T(8,128)S(1)} fusion(bf16[4096,288]{0,1:T(8,128)(2,1)S(1)} %copy-done, bf16[288,768]{0,1:T(8,128)(2,1)S(1)} %all_gather.19), kind=kOutput, calls=%fused_computation.15 | convolution fusion | flops 1811939328 | bytes 15384576 | tf_op jit(solution)/shard_map/dot_general | solution.py:12
  64.7 0.0 copy-start.2
  64.7 0.0 copy-start.5
  64.7 0.0 copy-start.8
  64.7 6.4 %fusion.7 = f32[4096,768]{1,0:T(8,128)} fusion(bf16[4096,288]{0,1:T(8,128)(2,1)S(1)} %copy-done, bf16[288,768]{0,1:T(8,128)(2,1)S(1)} %all_gather.20), kind=kOutput, calls=%fused_computation.16 | convolution fusion | flops 1811939328 | bytes 15384576 | tf_op jit(solution)/shard_map/dot_general | solution.py:11
  71.1 0.0 copy-done.5
  71.1 22.7 %all_gather.18 = bf16[768,288]{1,0:T(8,128)(2,1)S(1)} all-gather(bf16[24,288]{1,0:T(8,128)(2,1)S(1)} %copy-done.5), channel_id=1, replica_groups=mesh['dp'=4,'col'=4,'fsdp'=8] {'col','fsdp'}, dimensions={0}, use_global_device_ids=true | all-gather | bytes 456192 | tf_op jit(solution)/shard_map/all_gather | solution.py:33
  93.8 0.0 copy-done.2
  93.8 0.0 copy-done.8
  93.8 9.8 %fusion.4 = f32[1,288,768]{2,1,0:T(8,128)} fusion(bf16[4096,288]{0,1:T(8,128)(2,1)S(1)} %copy-done.8, f32[4096,768]{1,0:T(8,128)S(1)} %fusion.6, f32[4096,768]{1,0:T(8,128)} %fusion.7), kind=kOutput, calls=%fused_computation.10 | convolution fusion | flops 1830813696 | bytes 28409856 | tf_op jit(solution)/shard_map/td,tf->df/dot_general | solution.py:24
  103.6 17.0 %multiply_convert_fusion.1 = (bf16[4096,768]{1,0:T(8,128)(2,1)}, bf16[4096,768]{1,0:T(8,128)(2,1)}) fusion(f32[4096,768]{1,0:T(8,128)} %fusion.7, f32[4096,768]{1,0:T(8,128)} %copy-done.2, bf16[4096,288]{0,1:T(8,128)(2,1)S(1)} %copy-done.8, bf16[768,288]{1,0:T(8,128)(2,1)S(1)} %all_gather.18), kind=kOutput, calls=%fused_computation.1 | convolution fusion | flops 1852833792 | bytes 40550400 | tf_op jit(solution)/shard_map/td,fd->tf/dot_general | solution.py:16
  120.7 0.0 copy-start.3
  120.7 5.9 %convolution_bitcast_fusion.1 = f32[1,288,768]{2,1,0:T(8,128)} fusion(bf16[4096,288]{0,1:T(8,128)(2,1)S(1)} %copy-done, bf16[4096,768]{1,0:T(8,128)(2,1)} %get-tuple-element.13), kind=kOutput, calls=%fused_computation.12 | convolution fusion | flops 1811939328 | bytes 9535488 | tf_op jit(solution)/shard_map/td,tf->df/dot_general | solution.py:22
  126.6 0.0 copy-done.3
  126.6 0.0 copy-start.1
  126.6 4.3 %fusion.8 = f32[4096,288]{0,1:T(8,128)} fusion(bf16[4096,768]{1,0:T(8,128)(2,1)S(1)} %copy-done.3, bf16[288,768]{0,1:T(8,128)(2,1)S(1)} %all_gather.20), kind=kOutput, calls=%fused_computation.17 | convolution fusion | flops 1811939328 | bytes 11452416 | tf_op jit(solution)/shard_map/tf,df->td/dot_general | solution.py:19
  130.8 0.0 copy-done.1
  130.8 0.0 copy-start.6
  130.8 0.0 copy-start.9
  130.8 3.0 %convolution_bitcast_fusion = f32[1,288,768]{2,1,0:T(8,128)} fusion(bf16[4096,288]{0,1:T(8,128)(2,1)S(1)} %copy-done, bf16[4096,768]{1,0:T(8,128)(2,1)S(1)} %copy-done.1), kind=kOutput, calls=%fused_computation.11 | convolution fusion | flops 1811939328 | bytes 9535488 | tf_op jit(solution)/shard_map/td,tf->df/dot_general | solution.py:23
  133.9 0.0 copy-done.6
  133.9 24.2 %all_gather.21 = bf16[288,768]{0,1:T(8,128)(2,1)S(1)} all-gather(bf16[288,24]{0,1:T(8,128)(2,1)S(1)} %copy-done.6), channel_id=1, replica_groups=mesh['dp'=4,'col'=4,'fsdp'=8] {'col','fsdp'}, dimensions={1}, use_global_device_ids=true | all-gather | bytes 456192 | tf_op jit(solution)/shard_map/all_gather | solution.py:34
  158.1 1.0 copy.20
  159.1 22.7 %all_gather.22 = bf16[288,768]{0,1:T(8,128)(2,1)S(1)} all-gather(bf16[288,24]{0,1:T(8,128)(2,1)} %param.15), channel_id=1, replica_groups=mesh['dp'=4,'col'=4,'fsdp'=8] {'col','fsdp'}, dimensions={1}, use_global_device_ids=true | all-gather | bytes 456192 | tf_op jit(solution)/shard_map/all_gather | solution.py:35
  181.8 1.0 copy.21
  182.8 0.0 copy-done.9
  182.8 0.6 dynamic-slice
  184.0 3.4 %maximum_bitcast_fusion = f32[1,3,288,768]{3,2,1,0:T(8,128)} fusion(f32[1,288,768]{2,1,0:T(8,128)} %fusion.4, f32[1,288,768]{2,1,0:T(8,128)} %convolution_bitcast_fusion, f32[1,288,768]{2,1,0:T(8,128)} %convolution_bitcast_fusion.1), kind=kLoop, calls=%fused_computation.8 | loop fusion | flops 1327104 | bytes 5308416 | tf_op jit(solution)/shard_map/broadcast_in_dim | solution.py:40
  187.4 0.0 copy-start.7
  187.4 7.6 %fusion.2 = bf16[4096,288]{0,1:T(8,128)(2,1)} fusion(f32[4096,288]{0,1:T(8,128)} %fusion.8, bf16[4096,768]{1,0:T(8,128)(2,1)} %get-tuple-element.12, bf16[288,768]{0,1:T(8,128)(2,1)S(1)} %all_gather.19), kind=kOutput, calls=%fused_computation.7 | convolution fusion | flops 1814298624 | bytes 13811712 | tf_op jit(solution)/shard_map/tf,df->td/dot_general | solution.py:20
  195.0 0.0 all-reduce.6.cloned.1.call-done
  195.0 1.5 dynamic-slice_convert_fusion
  196.5 0.0 all-reduce.4.cloned.1.call-update
  196.5 0.0 copy-done.7
  196.5 24.2 %all_gather.23 = bf16[768,288]{1,0:T(8,128)(2,1)S(1)} all-gather(bf16[24,288]{1,0:T(8,128)(2,1)S(1)} %copy-done.7), channel_id=1, replica_groups=mesh['dp'=4,'col'=4,'fsdp'=8] {'col','fsdp'}, dimensions={0}, use_global_device_ids=true | all-gather | bytes 456192 | tf_op jit(solution)/shard_map/all_gather | solution.py:36
  220.7 1.0 copy.22
  221.7 13.2 %all-reduce.4.cloned.1.call-done = f32[3,288,24]{1,2,0:T(8,128)} async-done(((f32[3,288,24]{1,2,0:T(8,128)}), f32[3,288,24]{1,2,0:T(8,128)}) %all-reduce.4.cloned.1.call-update) | async-done | bytes 82960 | tf_op jit(solution)/shard_map/psum | solution.py:38
  235.0 1.5 copy.27
Async XLA Ops:
  7.2 54.0 %copy-start = (bf16[4096,288]{0,1:T(8,128)(2,1)S(1)}, bf16[4096,288]{0,1:T(8,128)(2,1)}, u32[]{:S(2)}) copy-start(bf16[4096,288]{0,1:T(8,128)(2,1)} %param.9) | copy-start | bytes 7077892
  7.2 29.8 %copy-start.4 = (bf16[288,24]{0,1:T(8,128)(2,1)S(1)}, bf16[288,24]{0,1:T(8,128)(2,1)}, u32[]{:S(2)}) copy-start(bf16[288,24]{0,1:T(8,128)(2,1)} %param.11) | copy-start | bytes 41476
  7.2 187.8 %all-reduce.6.cloned.1.call-start = ((), (), s32[]{:S(2)}) async-start(), calls=%async_computation.1 | async-start | bytes 3538944
  10.4 224.6 %all-reduce.4.cloned.1.call-start = ((), (), s32[]{:S(2)}) async-start(), calls=%async_computation | async-start | bytes 221184 | tf_op jit(solution)/shard_map/psum | solution.py:38
  64.7 29.1 %copy-start.2 = (f32[4096,768]{1,0:T(8,128)}, f32[4096,768]{1,0:T(8,128)S(1)}, u32[]{:S(2)}) copy-start(f32[4096,768]{1,0:T(8,128)S(1)} %fusion.6) | copy-start | bytes 37748740
  64.7 6.4 %copy-start.5 = (bf16[24,288]{1,0:T(8,128)(2,1)S(1)}, bf16[24,288]{1,0:T(8,128)(2,1)}, u32[]{:S(2)}) copy-start(bf16[24,288]{1,0:T(8,128)(2,1)} %param.13) | copy-start | bytes 41476
  64.7 29.1 %copy-start.8 = (bf16[4096,288]{0,1:T(8,128)(2,1)S(1)}, bf16[4096,288]{0,1:T(8,128)(2,1)}, u32[]{:S(2)}) copy-start(bf16[4096,288]{0,1:T(8,128)(2,1)} %param.10) | copy-start | bytes 7077892
  120.7 5.9 %copy-start.3 = (bf16[4096,768]{1,0:T(8,128)(2,1)S(1)}, bf16[4096,768]{1,0:T(8,128)(2,1)}, u32[]{:S(2)}) copy-start(bf16[4096,768]{1,0:T(8,128)(2,1)} %get-tuple-element.13) | copy-start | bytes 18874372
  126.6 4.3 %copy-start.1 = (bf16[4096,768]{1,0:T(8,128)(2,1)S(1)}, bf16[4096,768]{1,0:T(8,128)(2,1)}, u32[]{:S(2)}) copy-start(bf16[4096,768]{1,0:T(8,128)(2,1)} %get-tuple-element.12) | copy-start | bytes 18874372
  130.8 3.0 %copy-start.6 = (bf16[288,24]{0,1:T(8,128)(2,1)S(1)}, bf16[288,24]{0,1:T(8,128)(2,1)}, u32[]{:S(2)}) copy-start(bf16[288,24]{0,1:T(8,128)(2,1)} %param.14) | copy-start | bytes 41476
  130.8 51.9 %copy-start.9 = (u32[128]{0:T(128)S(1)}, u32[128]{0:T(128)}, u32[]{:S(2)}) copy-start(u32[128]{0:T(128)} %constant.11) | copy-start | bytes 1540
  187.4 9.1 %copy-start.7 = (bf16[24,288]{1,0:T(8,128)(2,1)S(1)}, bf16[24,288]{1,0:T(8,128)(2,1)}, u32[]{:S(2)}) copy-start(bf16[24,288]{1,0:T(8,128)(2,1)} %param.16) | copy-start | bytes 41476
Sparse Core Ops, SparseCore 0:
  11.4 110.2 all-reduce.5
  196.6 38.3 all-reduce.3
where the time goes:
time: 245 us; the launch traced here: 243 us
  blocking collectives  145 us (59%)
  matrix products  57.6 us (24%)
  between operations  14.8 us (6%)
  waiting for transfers between devices  13.3 us (5%)
  local copies, waits for them, and re-layouts  8.28 us (3%)
  other arithmetic  4.84 us (2%)
    all_gather x1, blocking collectives, device_step(): up_full = lax.all_gather(w_up, FSDP_AXES, axis=1, tiled=True)  26.6 us
    all_gather x1, blocking collectives, device_step(): v_down_full = lax.all_gather(v_down, FSDP_AXES, axis=0, tiled=True)  24.2 us
    all_gather x1, blocking collectives, device_step(): gate_full = lax.all_gather(w_gate, FSDP_AXES, axis=1, tiled=True)  24.2 us
    all_gather x1, blocking collectives, device_step(): v_gate_full = lax.all_gather(v_gate, FSDP_AXES, axis=1, tiled=True)  24.2 us
    all_gather x1, blocking collectives, device_step(): v_up_full = lax.all_gather(v_up, FSDP_AXES, axis=1, tiled=True)  22.7 us
    all_gather x1, blocking collectives, device_step(): down_full = lax.all_gather(w_down, FSDP_AXES, axis=0, tiled=True)  22.7 us
    dot_general x1, matrix products, local_backward(): jnp.einsum('td,fd->tf', dy_loc, down_full, preferred_element_type=jnp.flo...  17 us
    psum x1, waiting for transfers between devices, device_step(): grad_next = lax.psum(grad_shard.astype(jnp.float32), 'dp')  13.2 us
  transfers between devices with their start and end apart: 2, of which 1 were waited for; matrix products, arithmetic and copies ran while one was open for 27% of the time, Pallas kernels for 0%

commit v1 on v0

v1 whole, which is shorter than its diff:
```python
import functools

import jax
import jax.numpy as jnp
from jax import lax
from jax.experimental import pallas as pl
from jax.experimental.pallas import tpu as pltpu
from jax.sharding import PartitionSpec as P

ALL_AXES = ('dp', 'col', 'fsdp')
FSDP_AXES = ('col', 'fsdp')
F32, BF16 = jnp.float32, jnp.bfloat16
D, F, T = 288, 768, 4096
SH = 24
PK = 896
LA = 384
TB = 512
OFFS = (1, 3, 2)
MESH = pl.DeviceIdType.MESH


class Where:
    def __init__(self):
        self.z = lax.axis_index('dp')
        self.y = lax.axis_index('col')
        f = lax.axis_index('fsdp')
        self.x = lax.div(f, 2)
        self.c = lax.rem(f, 2)

    def xm(self, d):
        return lax.rem(self.x + 4 - d, 4)

    def ym(self, d):
        return lax.rem(self.y + 4 - d, 4)

    def to_x(self, d):
        return {'col': self.y, 'fsdp': lax.rem(self.x + d, 4) * 2 + self.c}

    def to_y(self, d):
        return {'col': lax.rem(self.y + d, 4), 'fsdp': self.x * 2 + self.c}

    def to_core(self):
        return {'col': self.y, 'fsdp': self.x * 2 + 1 - self.c}

    def to_z(self, d):
        return {'dp': lax.rem(self.z + d, 4)}


def rcopy(src, dst, ssem, rsem, dev):
    return pltpu.make_async_remote_copy(
        src_ref=src, dst_ref=dst, send_sem=ssem, recv_sem=rsem, device_id=dev, device_id_type=MESH)


def barrier(w):
    sem = pltpu.get_barrier_semaphore()
    devs = [w.to_core()] + [to(d) for d in OFFS for to in (w.to_x, w.to_y, w.to_z)]
    for dev in devs:
        pl.semaphore_signal(sem, inc=1, device_id=dev, device_id_type=MESH)
    pl.semaphore_wait(sem, len(devs))


class Gather:
    def __init__(self, w, buf, own_s, own_r, fa_s, fa_r, fb_s, fb_r, d_s, d_r):
        self.w, self.buf = w, buf
        self.own_s, self.own_r = own_s, own_r
        self.fa_s, self.fa_r, self.fb_s, self.fb_r = fa_s, fa_r, fb_s, fb_r
        self.d_s, self.d_r = d_s, d_r
        self.sent = []

    def piece(self, dx, dy, core=None):
        w = self.w
        return self.buf.at[w.ym(dy), w.xm(dx), w.c if core is None else core]

    def go(self, ref, ssem, rsem, dev):
        c = rcopy(ref, ref, ssem, rsem, dev)
        c.start()
        self.sent.append(c)

    def wait(self, ref, rsem):
        rcopy(ref, ref, rsem, rsem, self.w.to_core()).wait_recv()

    def share(self, dx, dy):
        self.go(self.piece(dx, dy), self.d_s.at[dx, dy], self.d_r.at[dx, dy], self.w.to_core())

    def start(self):
        me = self.piece(0, 0)
        for i, d in enumerate(OFFS):
            self.go(me, self.own_s.at[0, i], self.own_r.at[0, i], self.w.to_x(d))
            self.go(me, self.own_s.at[1, i], self.own_r.at[1, i], self.w.to_y(d))
        self.share(0, 0)

    def middle(self):
        w = self.w
        lo, hi = pl.ds(0, LA), pl.ds(LA, PK - LA)
        for i, d in enumerate(OFFS):
            p = self.piece(d, 0)
            self.wait(p, self.own_r.at[0, i])
            for j, e in enumerate(OFFS):
                self.go(p.at[:, lo], self.fa_s.at[i, j], self.fa_r.at[i, j], w.to_y(e))
            self.share(d, 0)
            p = self.piece(0, d)
            self.wait(p, self.own_r.at[1, i])
            for j, e in enumerate(OFFS):
                self.go(p.at[:, hi], self.fb_s.at[i, j], self.fb_r.at[i, j], w.to_x(e))
            self.share(0, d)

    def last(self):
        lo, hi = pl.ds(0, LA), pl.ds(LA, PK - LA)
        for i, dx in enumerate(OFFS):
            for j, dy in enumerate(OFFS):
                p = self.piece(dx, dy)
                self.wait(p.at[:, lo], self.fa_r.at[i, j])
                self.wait(p.at[:, hi], self.fb_r.at[j, i])
                self.share(dx, dy)

    def finish(self):
        for dx in range(4):
            for dy in range(4):
                self.wait(self.piece(dx, dy, 1 - self.w.c), self.d_r.at[dx, dy])

    def drain(self):
        for c in self.sent:
            c.wait_send()


def pack(dst, refs):
    for k, r in enumerate(refs):
        dst[:, 256 * k:256 * k + 256] = r[:, :256]
    rem = jnp.concatenate([r[:, 256:].astype(F32) for r in refs] + [jnp.zeros((SH, 32), F32)], axis=1)
    dst[:, 768:] = rem.astype(BF16)


def comm_kernel(wg, wu, wd, vg, vu, vd, g_hbm, gw_out, gv_out, dwn_out,
                gw, gv, gbuf, gt, rb0, cs, rb1a, rb1b, s1a, s1b, rb2a, rb2b, gz,
                ld_sem, st_sem,
                w0, w1, w2, w3, w4, w5, w6, w7, v0, v1, v2, v3, v4, v5, v6, v7,
                r0s, r0r, r1s, r1r, r2s, r2r, r3s, r3r):
    w = Where()
    load = pltpu.make_async_copy(g_hbm, gbuf, ld_sem)
    load.start()
    pack(gw.at[w.y, w.x, w.c], (wg, wu, wd))
    pack(gv.at[w.y, w.x, w.c], (vg, vu, vd))
    barrier(w)
    gather_w = Gather(w, gw, w0, w1, w2, w3, w4, w5, w6, w7)
    gather_v = Gather(w, gv, v0, v1, v2, v3, v4, v5, v6, v7)
    gather_w.start()

    load.wait()
    for m in range(7):
        if m < 6:
            blk = gbuf[m // 2, 128 * (m % 2):128 * (m % 2) + 128, :]
        else:
            blk = jnp.concatenate([gbuf[k, 256:, :] for k in range(3)] + [jnp.zeros((32, F), F32)], axis=0)
        t = blk.T
        for j in range(32):
            gt[j // 8, (j // 2) % 4, j % 2, :, 128 * m:128 * m + 128] = t[SH * j:SH * j + SH].astype(BF16)

    gather_w.middle()
    c0 = rcopy(gt.at[:, :, 1 - w.c], rb0, r0s, r0r, w.to_core())
    c0.start()
    gather_w.last()
    gather_w.finish()
    gather_w.drain()
    out_w = pltpu.make_async_copy(gw, gw_out, st_sem.at[0])
    out_w.start()
    gather_v.start()
    c0.wait()
    for y in range(4):
        for x in range(4):
            cs[y, x] = (gt[y, x, w.c].astype(F32) + rb0[y, x].astype(F32)).astype(BF16)
    sends = []
    lo, hi = pl.ds(0, LA), pl.ds(LA, PK - LA)
    for i, d in enumerate(OFFS):
        ca = rcopy(cs.at[:, lax.rem(w.x + d, 4), :, lo], rb1a.at[i], r1s.at[0, i], r1r.at[0, i], w.to_x(d))
        ca.start()
        cb = rcopy(cs.at[lax.rem(w.y + d, 4), :, :, hi], rb1b.at[i], r1s.at[1, i], r1r.at[1, i], w.to_y(d))
        cb.start()
        sends += [ca, cb]
    gather_v.middle()
    for c in sends:
        c.wait()
    for k in range(4):
        acc = cs[k, w.x, :, :LA].astype(F32)
        for i in range(3):
            acc += rb1a[i, k].astype(F32)
        s1a[k] = acc.astype(BF16)
        acc = cs[w.y, k, :, LA:].astype(F32)
        for i in range(3):
            acc += rb1b[i, k].astype(F32)
        s1b[k] = acc.astype(BF16)
    sends = []
    for i, d in enumerate(OFFS):
        ca = rcopy(s1a.at[lax.rem(w.y + d, 4)], rb2a.at[i], r2s.at[0, i], r2r.at[0, i], w.to_y(d))
        ca.start()
        cb = rcopy(s1b.at[lax.rem(w.x + d, 4)], rb2b.at[i], r2s.at[1, i], r2r.at[1, i], w.to_x(d))
        cb.start()
        sends += [ca, cb]
    gather_v.last()
    for c in sends:
        c.wait()
    acc = s1a[w.y].astype(F32)
    for i in range(3):
        acc += rb2a[i].astype(F32)
    gz[w.z, :, :LA] = acc.astype(BF16)
    acc = s1b[w.x].astype(F32)
    for i in range(3):
        acc += rb2b[i].astype(F32)
    gz[w.z, :, LA:] = acc.astype(BF16)
    gather_v.finish()
    sends = []
    for i, d in enumerate(OFFS):
        c = rcopy(gz.at[w.z], gz.at[w.z], r3s.at[i], r3r.at[i], w.to_z(d))
        c.start()
        sends.append(c)
    gather_v.drain()
    out_v = pltpu.make_async_copy(gv, gv_out, st_sem.at[1])
    out_v.start()
    for i, d in enumerate(OFFS):
        zm = gz.at[lax.rem(w.z + 4 - d, 4)]
        rcopy(zm, zm, r3s.at[i], r3r.at[i], w.to_core()).wait_recv()
    for c in sends:
        c.wait_send()
    tot = ((gz[0].astype(F32) + gz[1].astype(F32)) + gz[2].astype(F32)) + gz[3].astype(F32)
    for k in range(3):
        dwn_out[k, :, :256] = tot[:, 256 * k:256 * k + 256]
        dwn_out[k, :, 256:] = tot[:, 768 + 32 * k:800 + 32 * k]
    out_w.wait()
    out_v.wait()


def communicate(ws, vs, g):
    vmem = pl.BlockSpec(memory_space=pltpu.VMEM)
    hbm = pl.BlockSpec(memory_space=pl.ANY)
    dma = pltpu.SemaphoreType.DMA
    gsems = [dma((2, 3)), dma((2, 3)), dma((3, 3)), dma((3, 3)), dma((3, 3)), dma((3, 3)), dma((4, 4)), dma((4, 4))]
    full = (4, 4, 2, SH, PK)
    return pl.pallas_call(
        comm_kernel,
        out_shape=(jax.ShapeDtypeStruct(full, BF16), jax.ShapeDtypeStruct(full, BF16),
                   jax.ShapeDtypeStruct((3, SH, D), F32)),
        in_specs=[vmem] * 6 + [hbm],
        out_specs=(hbm, hbm, vmem),
        scratch_shapes=[
            pltpu.VMEM(full, BF16), pltpu.VMEM(full, BF16),
            pltpu.VMEM((3, D, F), F32), pltpu.VMEM(full, BF16),
            pltpu.VMEM((4, 4, SH, PK), BF16), pltpu.VMEM((4, 4, SH, PK), BF16),
            pltpu.VMEM((3, 4, SH, LA), BF16), pltpu.VMEM((3, 4, SH, PK - LA), BF16),
            pltpu.VMEM((4, SH, LA), BF16), pltpu.VMEM((4, SH, PK - LA), BF16),
            pltpu.VMEM((3, SH, LA), BF16), pltpu.VMEM((3, SH, PK - LA), BF16),
            pltpu.VMEM((4, SH, PK), BF16),
            dma, dma((2,)), *gsems, *gsems,
            dma, dma, dma((2, 3)), dma((2, 3)), dma((2, 3)), dma((2, 3)), dma((3,)), dma((3,)),
        ],
        compiler_params=pltpu.CompilerParams(collective_id=0, has_side_effects=True, vmem_limit_bytes=48 * 2**20),
        name="comm",
    )(*ws, *vs, g)


def mlp_kernel(xt, dyt, gw, gv, dxt, dw, vg, vu, vd, wcat, dcat):
    i = pl.program_id(0)

    @pl.when(i == 0)
    def _():
        rem = gw[:, 768:].T
        for k in range(2):
            wcat[:256, F * k:F * k + F] = gw[:, 256 * k:256 * k + 256].T
            wcat[256:, F * k:F * k + F] = rem[32 * k:32 * k + 32]
        rem = gv[:, 768:].T
        for k, o in enumerate((vg, vu, vd)):
            o[:256] = gv[:, 256 * k:256 * k + 256].T
            o[256:] = rem[32 * k:32 * k + 32]
        dw[...] = jnp.zeros_like(dw)

    dot = functools.partial(jnp.dot, preferred_element_type=F32)
    nt = lambda p, q: lax.dot_general(p, q, (((1,), (1,)), ((), ())), preferred_element_type=F32)
    x, dy = xt[...], dyt[...]
    zero = jnp.zeros((32, TB), BF16)
    wr = gw[:, 768:]

    def up(k, t):
        rem = [zero] * 4
        rem[k] = t[256:]
        return dot(gw[:, 256 * k:256 * k + 256], t[:256]) + dot(wr, jnp.concatenate(rem, axis=0))

    a = up(0, x)
    b = up(1, x)
    dh = up(2, dy)
    s = jax.nn.sigmoid(a)
    act = a * s
    h = (act * b).astype(BF16)
    dg = (dh * b * (s + act * (1.0 - s))).astype(BF16)
    du = (dh * act).astype(BF16)
    dcat[:F] = dg
    dcat[F:] = du
    dxt[...] = dot(wcat[...], dcat[...]).astype(BF16)
    dw[0] += nt(x, dg)
    dw[1] += nt(x, du)
    dw[2] += nt(dy, h)


def mlp(xt, dyt, gw, gv):
    full = lambda *s: pl.BlockSpec(s, lambda i: (0,) * len(s))
    tok = pl.BlockSpec((D, TB), lambda i: (0, i))
    return pl.pallas_call(
        mlp_kernel, grid=(T // TB,),
        out_shape=(jax.ShapeDtypeStruct((D, T), BF16), jax.ShapeDtypeStruct((3, D, F), F32),
                   *[jax.ShapeDtypeStruct((D, F), BF16)] * 3),
        in_specs=[tok, tok, full(F, PK), full(F, PK)],
        out_specs=(tok, full(3, D, F), full(D, F), full(D, F), full(D, F)),
        scratch_shapes=[pltpu.VMEM((D, 2 * F), BF16), pltpu.VMEM((2 * F, TB), BF16)],
        compiler_params=pltpu.CompilerParams(dimension_semantics=("arbitrary",), vmem_limit_bytes=48 * 2**20),
        name="mlp",
    )(xt, dyt, gw, gv)


def solution(mesh):
    def device_step(x_loc, dy_loc, w_gate, w_up, w_down, v_gate, v_up, v_down, g_next):
        gw, gv, dwn = communicate((w_gate.T, w_up.T, w_down), (v_gate.T, v_up.T, v_down), g_next[0])
        dxt, dw, vg, vu, vd = mlp(x_loc.T, dy_loc.T, gw.reshape(F, PK), gv.reshape(F, PK))
        return dxt.T, dwn.transpose(0, 2, 1), dw[None], vg, vu, vd.T

    row_spec = P(ALL_AXES, None)
    col_shard = P(None, FSDP_AXES)
    row_shard = P(FSDP_AXES, None)
    dev_spec = P(ALL_AXES, None, None, None)
    return jax.shard_map(
        device_step, mesh=mesh,
        in_specs=(row_spec, row_spec, col_shard, col_shard, row_shard, col_shard, col_shard, row_shard, dev_spec),
        out_specs=(row_spec, P(None, None, FSDP_AXES), dev_spec, P(), P(), P()),
        check_vma=False)
```

time: 245 us -> 70.8 us (0.29)
  blocking collectives: 145 us -> 0 us
  Pallas kernels: 0 us -> 63 us
  matrix products: 57.6 us -> 0 us
  between operations: 14.8 us -> 0.67 us
  waiting for transfers between devices: 13.3 us -> 0 us
  other arithmetic: 4.84 us -> 0 us
    all_gather x6 -> x0, blocking collectives: 145 us -> none  [the longest x1 26.6 us: device_step(): up_full = lax.all_gather(w_up, FSDP_AXES, axis=1, tiled=True)]
    pallas_call x0 -> x2, Pallas kernels: none -> 63 us  [the longest x1 36.9 us: communicate(): pl.pallas_call(comm_kernel, out_shape=(jax.ShapeDtypeStruct(full, BF16),...]
    dot_general x8 -> x0, matrix products: 57.6 us -> none  [the longest x1 17 us: local_backward(): jnp.einsum('td,fd->tf', dy_loc, down_full, preferred_element_type=jnp.flo...]
    psum x1 -> x0, waiting for transfers between devices: 13.2 us -> none  [device_step(): grad_next = lax.psum(grad_shard.astype(jnp.float32), 'dp')]
    broadcast_in_dim x1 -> x0, other arithmetic: 3.37 us -> none  [device_step(): grad_local[None]]
    unnamed x26 -> x17, local copies, waits for them, and re-layouts: 8.28 us -> 6.72 us
  transfers between devices with their start and end apart: 2 -> 0, of which waited for: 1 -> 0; matrix products, arithmetic and copies ran while one was open for 27% -> 0% of each run, Pallas kernels for 0% -> 0%
where the time goes in v1:
time: 70.8 us; the launch traced here: 70.4 us
  Pallas kernels  63 us (89%)
  local copies, waits for them, and re-layouts  6.72 us (9%)
    pallas_call x1, Pallas kernels, communicate(): pl.pallas_call(comm_kernel, out_shape=(jax.ShapeDtypeStruct(full, BF16),...  36.9 us
    pallas_call x1, Pallas kernels, mlp(): pl.pallas_call(mlp_kernel, grid=(T // TB,), out_shape=(jax.ShapeDtypeStru...  26.1 us
    unnamed x17, local copies, waits for them, and re-layouts  6.72 us

profile of v1, /device:TPU:1, one launch (start us, length us, event | category | flops | bytes accessed | tf_op | source)
XLA Modules:
  0.0 70.4 jit_solution(18151885879214020926)
XLA Ops:
  0.6 0.0 copy-start
  0.6 1.7 %copy-done = f32[1,3,288,768]{3,2,1,0:T(8,128)S(1)} copy-done((f32[1,3,288,768]{3,2,1,0:T(8,128)S(1)}, f32[1,3,288,768]{3,2,1,0:T(8,128)}, u32[]{:S(2)}) %copy-start) | copy-done | bytes 2654232
  2.4 0.0 copy-start.2
  2.4 0.7 %copy-done.2 = bf16[288,24]{0,1:T(8,128)(2,1)S(1)} copy-done((bf16[288,24]{0,1:T(8,128)(2,1)S(1)}, bf16[288,24]{0,1:T(8,128)(2,1)}, u32[]{:S(2)}) %copy-start.2) | copy-done | bytes 13848
  3.1 0.0 copy-start.3
  3.1 0.7 %copy-done.3 = bf16[288,24]{0,1:T(8,128)(2,1)S(1)} copy-done((bf16[288,24]{0,1:T(8,128)(2,1)S(1)}, bf16[288,24]{0,1:T(8,128)(2,1)}, u32[]{:S(2)}) %copy-start.3) | copy-done | bytes 13848
  3.8 0.0 copy-start.4
  3.8 0.7 %copy-done.4 = bf16[24,288]{1,0:T(8,128)(2,1)S(1)} copy-done((bf16[24,288]{1,0:T(8,128)(2,1)S(1)}, bf16[24,288]{1,0:T(8,128)(2,1)}, u32[]{:S(2)}) %copy-start.4) | copy-done | bytes 13848
  4.6 0.0 copy-start.5
  4.6 0.7 %copy-done.5 = bf16[288,24]{0,1:T(8,128)(2,1)S(1)} copy-done((bf16[288,24]{0,1:T(8,128)(2,1)S(1)}, bf16[288,24]{0,1:T(8,128)(2,1)}, u32[]{:S(2)}) %copy-start.5) | copy-done | bytes 13848
  5.3 0.0 copy-start.6
  5.3 0.7 %copy-done.6 = bf16[288,24]{0,1:T(8,128)(2,1)S(1)} copy-done((bf16[288,24]{0,1:T(8,128)(2,1)S(1)}, bf16[288,24]{0,1:T(8,128)(2,1)}, u32[]{:S(2)}) %copy-start.6) | copy-done | bytes 13848
  6.0 0.0 copy-start.7
  6.0 0.7 %copy-done.7 = bf16[24,288]{1,0:T(8,128)(2,1)S(1)} copy-done((bf16[24,288]{1,0:T(8,128)(2,1)S(1)}, bf16[24,288]{1,0:T(8,128)(2,1)}, u32[]{:S(2)}) %copy-start.7) | copy-done | bytes 13848
  6.7 0.0 copy-start.1
  6.7 36.9 %comm.1 = (bf16[4,4,2,24,896]{4,3,2,1,0:T(8,128)(2,1)S(1)}, bf16[4,4,2,24,896]{4,3,2,1,0:T(8,128)(2,1)S(1)}, f32[3,24,288]{2,1,0:T(8,128)S(1)}) custom-call(bf16[24,288]{1,0:T(8,128)(2,1)S(1)} %bitcast.18, bf16[24,288]{1,0:T(8,128)(2,1)S(1)} %bitcast.19, bf16[24,288]{1,0:T(8,128)(2,1)S(1)} %copy-done.4, bf16[24,288]{1,0:T(8,128)(2,1)S(1)} %bitcast.20, ...), custom_call_target="tpu_custom_call" | custom-call | tf_op jit(solution)/shard_map/comm/pallas_call | solution.py:237
  43.6 0.0 copy-done.1
  43.6 26.1 %mlp.1 = (bf16[288,4096]{1,0:T(8,128)(2,1)}, f32[3,288,768]{2,1,0:T(8,128)}, bf16[288,768]{1,0:T(8,128)(2,1)}, bf16[288,768]{1,0:T(8,128)(2,1)}, bf16[288,768]{1,0:T(8,128)(2,1)}) custom-call(bf16[288,4096]{1,0:T(8,128)(2,1)S(1)} %bitcast.14, bf16[288,4096]{1,0:T(8,128)(2,1)} %bitcast.22, bf16[768,896]{1,0:T(8,128)(2,1)S(1)} %bitcast.15, ...), custom_call_target="tpu_custom_call" | custom-call | tf_op jit(solution)/shard_map/mlp/pallas_call | solution.py:304
  69.7 0.6 copy.16
Async XLA Ops:
  0.6 1.8 %copy-start = (f32[1,3,288,768]{3,2,1,0:T(8,128)S(1)}, f32[1,3,288,768]{3,2,1,0:T(8,128)}, u32[]{:S(2)}) copy-start(f32[1,3,288,768]{3,2,1,0:T(8,128)} %param.17) | copy-start | bytes 7962628
  2.4 0.7 %copy-start.2 = (bf16[288,24]{0,1:T(8,128)(2,1)S(1)}, bf16[288,24]{0,1:T(8,128)(2,1)}, u32[]{:S(2)}) copy-start(bf16[288,24]{0,1:T(8,128)(2,1)} %param.11) | copy-start | bytes 41476
  3.1 0.7 %copy-start.3 = (bf16[288,24]{0,1:T(8,128)(2,1)S(1)}, bf16[288,24]{0,1:T(8,128)(2,1)}, u32[]{:S(2)}) copy-start(bf16[288,24]{0,1:T(8,128)(2,1)} %param.12) | copy-start | bytes 41476
  3.8 0.7 %copy-start.4 = (bf16[24,288]{1,0:T(8,128)(2,1)S(1)}, bf16[24,288]{1,0:T(8,128)(2,1)}, u32[]{:S(2)}) copy-start(bf16[24,288]{1,0:T(8,128)(2,1)} %wd.1) | copy-start | bytes 41476
  4.6 0.7 %copy-start.5 = (bf16[288,24]{0,1:T(8,128)(2,1)S(1)}, bf16[288,24]{0,1:T(8,128)(2,1)}, u32[]{:S(2)}) copy-start(bf16[288,24]{0,1:T(8,128)(2,1)} %param.14) | copy-start | bytes 41476
  5.3 0.7 %copy-start.6 = (bf16[288,24]{0,1:T(8,128)(2,1)S(1)}, bf16[288,24]{0,1:T(8,128)(2,1)}, u32[]{:S(2)}) copy-start(bf16[288,24]{0,1:T(8,128)(2,1)} %param.15) | copy-start | bytes 41476
  6.0 0.7 %copy-start.7 = (bf16[24,288]{1,0:T(8,128)(2,1)S(1)}, bf16[24,288]{1,0:T(8,128)(2,1)}, u32[]{:S(2)}) copy-start(bf16[24,288]{1,0:T(8,128)(2,1)} %vd.1) | copy-start | bytes 41476
  6.7 36.9 %copy-start.1 = (bf16[4096,288]{0,1:T(8,128)(2,1)S(1)}, bf16[4096,288]{0,1:T(8,128)(2,1)}, u32[]{:S(2)}) copy-start(bf16[4096,288]{0,1:T(8,128)(2,1)} %param.9) | copy-start | bytes 7077892
